TPU v7x, 768 devices: a whole 4x8x12 slice. The times are simulated.
768 devices in a mesh: gx: 96 (over x, z, core), gy: 8 (over y).
Axes of the slice: x: 4, y: 8, z: 12, core: 2. Of those that a mesh axis runs over, the one named last changes fastest.
Arguments:
- coarse_state: float32 [5, 3072, 2048], P(None, 'gx', 'gy'), may hold values from -6 to 6
- fine_state: float32 [768, 5, 32, 512], P(('gx', 'gy')), may hold values from -6 to 6
- slot_site: int32 [768, 2], P(('gx', 'gy')), may hold values from 0 to 7, as said below
- box_live: int32 [768], P(('gx', 'gy')), may hold values 0 or 1
Outputs:
- coarse_out: float32 [5, 3072, 2048], P(None, 'gx', 'gy')
- fine_out: float32 [768, 5, 32, 512], P(('gx', 'gy'))
Inputs may be any that keep to these rules, and one draw needn't show every extreme that they name: `slot_site`: within each group of 8 devices that share a gx index, slots of the group and box positions of the group's coarse blocks are matched one to one; column 0 is the gy index of the block, column 1 the position number, 0 to 0.
All inputs are finite; a program needn't handle non-finite values. No bound on the sum of `box_live` on one device may be relied on, other than what follows from the above.
Results may differ from a plain program's by a relative error of at most 0.000088.
Values sent between devices are 32-bit elements; how exact they have to be, the bound alone decides.
A program may use at most 64 MiB of HBM per device.

v0:
```python
import jax
import jax.numpy as jnp
from jax import lax
from jax.experimental import pallas as pl
from jax.experimental.pallas import tpu as pltpu
from jax.sharding import PartitionSpec as P

NV = 5
GY = 8
courant = 0.2
drift = (0.5, 0.3, 0.2)
signal = (1.5, 1.3, 1.2)
MESH = pl.DeviceIdType.MESH
F32 = jnp.float32


def iota(shape, dim):
    return lax.broadcasted_iota(jnp.int32, shape, dim)


def up(x, n, axis):
    return pltpu.roll(x, x.shape[axis] - n, axis)


def down(x, n, axis):
    return pltpu.roll(x, n, axis)


def z_up(x, depth):
    last = iota(x.shape, 1) % depth == depth - 1
    return jnp.where(last, pltpu.roll(x, depth - 1, 1), pltpu.roll(x, 127, 1))


def z_down(x, depth):
    first = iota(x.shape, 1) % depth == 0
    return jnp.where(first, pltpu.roll(x, 129 - depth, 1), pltpu.roll(x, 1, 1))


def minmod(a, b):
    return jnp.maximum(jnp.minimum(a, b), 0.0) + jnp.minimum(jnp.maximum(a, b), 0.0)


def face_fluxes(q, d, ahead, behind):
    plus = 0.5 * (drift[d] + signal[d])
    minus = 0.5 * (drift[d] - signal[d])
    left, right = [], []
    for v in q:
        diff = ahead(v) - v
        half = 0.5 * minmod(behind(diff), diff)
        left.append(v + half)
        right.append(v - half)

    def side(s, coef):
        vn = 0.5 * s[1 + d]
        out = [coef * x for x in s]
        out[0] = out[0] + vn
        out[4] = out[4] + vn
        out[1 + d] = out[1 + d] + 0.5 * s[4]
        return out

    a, b = side(left, plus), side(right, minus)
    return [x + ahead(y) for x, y in zip(a, b)]


def z_pass(q_ref, out_ref, width, depth):
    for t in range(width // 128):
        lanes = pl.ds(128 * t, 128)
        q = [q_ref[m, 0:32, lanes] for m in range(NV)]
        f = face_fluxes(q, 2, lambda x: z_up(x, depth), lambda x: z_down(x, depth))
        for m in range(NV):
            out_ref[m, :, lanes] = f[m] - z_down(f[m], depth)


def x_pass(q_ref, out_ref, width, keep):
    for t in range(width // 128):
        lanes = pl.ds(128 * t, 128)
        q = [q_ref[m, :, lanes] for m in range(NV)]
        f = face_fluxes(q, 0, lambda x: up(x, 1, 0), lambda x: down(x, 1, 0))
        for m in range(NV):
            low = down(f[m], 1, 0)
            out_ref[m, :, lanes] = (f[m] - low)[0:32]
            keep(m, lanes, f[m], low)


def y_pass(q_ref, width, depth, emit, keep):
    for r in range(4):
        rows = pl.ds(8 * r, 8)
        q = [q_ref[m, rows, :] for m in range(NV)]
        f = face_fluxes(q, 1, lambda x: up(x, depth, 1), lambda x: down(x, depth, 1))
        for m in range(NV):
            low = down(f[m], depth, 1)
            keep(m, r, f[m], low)
            emit(m, r, q[m][:, 0:width], (f[m] - low)[:, 0:width])


def dot(a, b):
    return jnp.dot(a, b, precision=lax.Precision.HIGHEST, preferred_element_type=F32)


def kernel(
    coarse, fine, site_ref, live_ref, coarse_out, fine_out,
    cq, fq, cz, cx, cn, fz, fx, cflx, cfly, xf, yf, ps,
    spread_x, spread_y, gather_x, gather_y, ring, mids, pieces, stage, order, arrived,
    hxs, hxr, hys, hyr,
    in_sem, out_sem, ring_s, ring_r, mid_s, mid_r, one_s, one_r, two_s, two_r, hal_s, hal_r,
):
    gx, gy = lax.axis_index("gx"), lax.axis_index("gy")
    ngx = lax.axis_size("gx")
    site = site_ref[0, 0]
    live = live_ref[0]

    load_c = pltpu.make_async_copy(coarse, cq.at[:, 0:32, 0:256], in_sem.at[0])
    load_f = pltpu.make_async_copy(fine, fq.at[:, 0:32, 0:512], in_sem.at[1])
    load_c.start()
    load_f.start()
    barrier = pltpu.get_barrier_semaphore()
    gx_lo, gx_hi = lax.rem(gx + ngx - 1, ngx), lax.rem(gx + 1, ngx)
    for g in (gx_lo, gx_hi):
        pl.semaphore_signal(barrier, inc=1, device_id=(g, gy), device_id_type=MESH)
    far = (4, 3, 5, 2, 6, 1, 7)
    peers = [lax.rem(gy + k, GY) for k in far]
    for p in peers:
        pl.semaphore_signal(barrier, inc=1, device_id=(gx, p), device_id_type=MESH)

    k, o = iota((128, 512), 0), iota((128, 512), 1)
    spread_x[...] = jnp.where(k == (o // 32) * 8 + (o % 16) // 2, 1.0, 0.0)
    k, o = iota((256, 128), 0), iota((256, 128), 1)
    hit = (k % 8 == (o % 16) // 2) & (((k < 128) & (o >= 96)) | ((k >= 128) & (o < 32)))
    spread_y[...] = jnp.where(hit, 1.0, 0.0)
    k, o = iota((512, 128), 0), iota((512, 128), 1)
    gather_x[...] = jnp.where(o == (k // 32) * 8 + (k % 16) // 2, 0.125, 0.0)
    k, o = iota((128, 128), 0), iota((128, 128), 1)
    gather_y[...] = jnp.where((k >= 112) & ((k % 16) // 2 == o % 8), 0.125, 0.0)
    pick_low = jnp.where(k == 56 + o % 8, 1.0, 0.0)
    pick_high = jnp.where(k == 64 + o % 8, 1.0, 0.0)

    cq[:, 32:40, :] = jnp.zeros((NV, 8, 384), F32)
    cq[:, 0:32, 256:384] = jnp.zeros((NV, 32, 128), F32)
    fq[:, 32:40, :] = jnp.zeros((NV, 8, 640), F32)
    xf[...] = jnp.zeros((16, 512), F32)

    lane16 = iota((16, 128), 1)
    own = lane16 // 8 == iota((16, 128), 0)

    def put_ring(dst, get):
        for m in range(NV):
            for face, row in ((0, 7), (1, 24)):
                first, second = get(m, row, row + 1, 0), get(m, row, row + 1, 1)
                both = jnp.where(
                    iota((1, 128), 1) < 64, pltpu.roll(first, 64, 1), pltpu.roll(second, 64, 1)
                )
                dst[gy, 5 * face + m : 5 * face + m + 1, :] = both
        for face, pick in ((2, pick_low), (3, pick_high)):
            cols = jnp.concatenate([get(m, 8, 24, face - 2) for m in range(NV)], axis=0)
            copies = dot(cols, pick)
            for m in range(NV):
                part = jnp.where(own, copies[16 * m : 16 * m + 16], 0.0)
                dst[gy, 5 * face + m : 5 * face + m + 1, :] = jnp.sum(part, axis=0, keepdims=True)

    load_c.wait()
    ring[gy, 16:24, :] = jnp.full((8, 128), site, jnp.int32).astype(F32)
    put_ring(ring, lambda m, a, b, t: cq[m, a:b, 128 * t : 128 * t + 128])
    for m in range(NV):
        hxs[0, 2 * m : 2 * m + 2, :] = cq[m, 0:2, 0:256]
        hxs[1, 2 * m : 2 * m + 2, :] = cq[m, 30:32, 0:256]
    lane8 = iota((8, 128), 1)
    for side, tile, base in ((0, 0, 0), (1, 1, 112)):
        for g in range(3):
            acc = jnp.zeros((8, 128), F32)
            for n in range(8 * g, min(8 * g + 8, 20)):
                block = cq[n // 4, 8 * (n % 4) : 8 * (n % 4) + 8, 128 * tile : 128 * tile + 128]
                moved = pltpu.roll(block, (16 * (n % 8) - base) % 128, 1) if (16 * (n % 8) - base) % 128 else block
                acc = jnp.where(lane8 // 16 == n % 8, moved, acc)
            hys[side, g] = acc

    def spread(buf, sends, recvs):
        out = []
        for i, p in enumerate(peers):
            c = pltpu.make_async_remote_copy(
                src_ref=buf.at[gy], dst_ref=buf.at[gy], send_sem=sends.at[i], recv_sem=recvs.at[gy],
                device_id=(gx, p), device_id_type=MESH,
            )
            c.start()
            out.append(c)
        return out

    def received(buf, sends, recvs):
        for i, k in enumerate(far):
            src = lax.rem(gy + GY - k, GY)
            pltpu.make_async_remote_copy(
                src_ref=buf.at[src], dst_ref=buf.at[src], send_sem=sends.at[i], recv_sem=recvs.at[src],
                device_id=(gx, src), device_id_type=MESH,
            ).wait_recv()

    pl.semaphore_wait(barrier, 9)
    pending = spread(ring, ring_s, ring_r)

    def coarse_keep_x(m, lanes, f, low):
        cflx[m, 0, :, lanes] = f[0:8]
        cflx[m, 1, :, lanes] = low[24:32]

    def coarse_keep_y(m, r, f, low):
        if r in (1, 2):
            cfly[m, 0, 8 * (r - 1) : 8 * r, :] = f[:, 0:128]
            cfly[m, 1, 8 * (r - 1) : 8 * r, :] = low[:, 128:256]

    def coarse_emit(m, r, q, div):
        rows = pl.ds(8 * r, 8)
        cn[m, rows, :] = q - courant * (cx[m, rows, :] + cz[m, rows, :] + div)

    z_pass(cq, cz, 256, 8)
    x_pass(cq, cx, 256, coarse_keep_x)
    y_pass(cq, 256, 8, coarse_emit, coarse_keep_y)
    put_ring(
        mids,
        lambda m, a, b, t: 0.5
        * (cq[m, a:b, 128 * t : 128 * t + 128] + cn[m, a:b, 128 * t : 128 * t + 128]),
    )
    pending += spread(mids, mid_s, mid_r)

    gy_lo, gy_hi = lax.rem(gy + GY - 1, GY), lax.rem(gy + 1, GY)
    for i, (src, dst, where) in enumerate(
        (
            (hxs.at[0], hxr.at[0], (gx_lo, gy)),
            (hxs.at[1], hxr.at[1], (gx_hi, gy)),
            (hys.at[0], hyr.at[0], (gx, gy_lo)),
            (hys.at[1], hyr.at[1], (gx, gy_hi)),
        )
    ):
        c = pltpu.make_async_remote_copy(
            src_ref=src, dst_ref=dst, send_sem=hal_s.at[i], recv_sem=hal_r.at[i],
            device_id=where, device_id_type=MESH,
        )
        c.start()
        pending.append(c)
    halo = pending[-4:]

    site_v = jnp.full((24, 128), site, jnp.int32)
    row32 = iota((32, 128), 0)
    mine = iota((32, 128), 1) // 8 == row32 // 2

    def ghosts(buf):
        got = jnp.zeros((24, 128), F32)
        for s in range(GY):
            got = jnp.where(site_v == s, buf[s], got)
        wide = dot(got[0:16], spread_x[...])
        lows = jnp.concatenate([jnp.where(mine, got[10 + m : 11 + m], 0.0) for m in range(NV)], axis=0)
        highs = jnp.concatenate([jnp.where(mine, got[15 + m : 16 + m], 0.0) for m in range(NV)], axis=0)
        side = dot(jnp.concatenate([lows, highs], axis=1), spread_y[...])
        edge = iota((8, 512), 0) < 4
        for m in range(NV):
            fq[m, 32:40, 0:512] = jnp.where(edge, wide[5 + m : 6 + m], wide[m : m + 1])
            fq[m, 0:32, 512:640] = side[32 * m : 32 * m + 32]

    def fine_step(first):
        def keep_x(m, lanes, f, low):
            if first:
                xf[m : m + 1, lanes] = f[39:40]
                xf[5 + m : 6 + m, lanes] = f[31:32]
            else:
                xf[m : m + 1, lanes] += f[39:40]
                xf[5 + m : 6 + m, lanes] += f[31:32]

        def keep_y(m, r, f, low):
            at = 64 * m + 8 * r
            if first:
                yf[at : at + 8, :] = f[:, 512:640]
                yf[at + 32 : at + 40, :] = f[:, 384:512]
            else:
                yf[at : at + 8, :] += f[:, 512:640]
                yf[at + 32 : at + 40, :] += f[:, 384:512]

        def emit(m, r, q, div):
            rows = pl.ds(8 * r, 8)
            new = q - courant * (fx[m, rows, :] + fz[m, rows, :] + div)
            fq[m, rows, 0:512] = new
            if not first:
                for t in range(4):
                    ps[t, 32 * m + 8 * r : 32 * m + 8 * r + 8, :] = new[:, 128 * t : 128 * t + 128]

        x_pass(fq, fx, 512, keep_x)
        y_pass(fq, 512, 16, emit, keep_y)

    load_f.wait()
    z_pass(fq, fz, 512, 16)
    received(ring, ring_s, ring_r)
    ghosts(ring)
    fine_step(True)
    z_pass(fq, fz, 512, 16)
    received(mids, mid_s, mid_r)
    ghosts(mids)
    fine_step(False)
    store_f = pltpu.make_async_copy(fq.at[:, 0:32, 0:512], fine_out, out_sem.at[0])
    store_f.start()

    pairs = jnp.concatenate(
        [ps[t, pl.ds(0, 80, stride=2), :] + ps[t, pl.ds(1, 80, stride=2), :] for t in range(4)], axis=1
    )
    means = dot(jnp.concatenate([pairs, xf[...]], axis=0), gather_x[...])
    for a in range(6):
        pieces[a] = means[16 * a : 16 * a + 16]
    cols = dot(yf[pl.ds(0, 160, stride=2), :] + yf[pl.ds(1, 160, stride=2), :], gather_y[...])
    acc = jnp.zeros((16, 128), F32)
    for n in range(10):
        acc = jnp.where(lane16 // 8 == n, cols[16 * n : 16 * n + 16], acc)
    pieces[6] = acc

    def exchange_one(i, p, s):
        return pltpu.make_async_remote_copy(
            src_ref=pieces.at[p], dst_ref=stage.at[s], send_sem=one_s.at[i], recv_sem=one_r.at[s],
            device_id=(gx, p), device_id_type=MESH,
        )

    def exchange_two(i, p, s):
        return pltpu.make_async_remote_copy(
            src_ref=order.at[p], dst_ref=arrived.at[s], send_sem=two_s.at[i], recv_sem=two_r.at[s],
            device_id=(gx, p), device_id_type=MESH,
        )

    for i, p in enumerate(peers):
        @pl.when(p != GY - 1)
        def _():
            exchange_one(i, p, gy).start()

    stage[gy] = pieces[gy]

    for c in halo:
        c.wait_recv()
    for m in range(NV):
        two = jnp.concatenate([hxr[0, 2 * m : 2 * m + 2, :], jnp.zeros((4, 256), F32), hxr[1, 2 * m : 2 * m + 2, :]], axis=0)
        cq[m, 32:40, 0:256] = two
        for r in range(4):
            n = 4 * m + r
            high = pltpu.roll(hyr[0, n // 8], (-16 * (n % 8)) % 128, 1) if n % 8 else hyr[0, n // 8]
            low = pltpu.roll(hyr[1, n // 8], (112 - 16 * (n % 8)) % 128, 1) if n % 8 != 7 else hyr[1, n // 8]
            cq[m, 8 * r : 8 * r + 8, 256:384] = jnp.where(
                lane8 < 16, high, jnp.where(lane8 >= 112, low, 0.0)
            )
    x_pass(cq, cx, 256, coarse_keep_x)
    y_pass(cq, 256, 8, coarse_emit, coarse_keep_y)

    weight = jnp.full((16, 128), live, jnp.int32).astype(F32) * courant
    w8 = weight[0:8]
    present = jnp.full((16, 128), live, jnp.int32) > 0
    row8 = iota((8, 128), 0)

    @pl.when(gy != GY - 1)
    def _():
        for i, k in enumerate(far):
            exchange_one(i, gy, lax.rem(gy + GY - k, GY)).wait_recv()
        tags = [jnp.broadcast_to(ring[s, 23:24, :], (16, 128)) for s in range(GY)]
        for d in range(GY):
            acc = jnp.zeros((16, 128), F32)
            for s in range(GY):
                acc = jnp.where(tags[s] == float(d), stage[s], acc)
            order[d] = acc
        for i, p in enumerate(peers):
            exchange_two(i, p, gy).start()
        arrived[gy] = order[gy]

    for i, k in enumerate(far):
        src = lax.rem(gy + GY - k, GY)

        @pl.when(src != GY - 1)
        def _():
            exchange_two(i, src, src).wait_recv()

    for m in range(NV):
        mean = pltpu.roll(arrived[m], 64, 1)
        left = cn[m, 8:24, 0:128]
        right = cn[m, 8:24, 128:256]
        left = jnp.where(present & (lane16 >= 64), mean, left)
        right = jnp.where(present & (lane16 < 64), mean, right)
        low = pltpu.roll(arrived[6], (56 - 16 * m) % 128, 1)
        high = pltpu.roll(arrived[6], (56 - 16 * m) % 128, 1)
        left = left + jnp.where(lane16 // 8 == 7, weight * (cfly[m, 0] - low), 0.0)
        right = right + jnp.where(lane16 // 8 == 8, weight * (high - cfly[m, 1]), 0.0)
        cn[m, 8:24, 0:128] = left
        cn[m, 8:24, 128:256] = right
        low = jnp.broadcast_to(pltpu.roll(arrived[5, m : m + 1, :], 64, 1), (8, 128))
        high = jnp.broadcast_to(pltpu.roll(arrived[5, 5 + m : 6 + m, :], 64, 1), (8, 128))
        for t in range(2):
            lanes = pl.ds(128 * t, 128)
            inside = lane8 >= 64 if t == 0 else lane8 < 64
            cn[m, 0:8, lanes] += jnp.where(inside & (row8 == 7), w8 * (cflx[m, 0, :, lanes] - low), 0.0)
            cn[m, 24:32, lanes] += jnp.where(inside & (row8 == 0), w8 * (high - cflx[m, 1, :, lanes]), 0.0)

    store_c = pltpu.make_async_copy(cn, coarse_out, out_sem.at[1])
    store_c.start()
    for c in pending:
        c.wait_send()
    for i, p in enumerate(peers):
        @pl.when(p != GY - 1)
        def _():
            exchange_one(i, p, gy).wait_send()

    @pl.when(gy != GY - 1)
    def _():
        for i, p in enumerate(peers):
            exchange_two(i, p, gy).wait_send()

    store_f.wait()
    store_c.wait()


def shards(coarse_state, fine_state, slot_site, box_live):
    dma = pltpu.SemaphoreType.DMA
    vm = lambda *s: pltpu.VMEM(s, F32)
    coarse_out, fine_out = pl.pallas_call(
        kernel,
        out_shape=(
            jax.ShapeDtypeStruct((NV, 32, 256), F32),
            jax.ShapeDtypeStruct((NV, 32, 512), F32),
        ),
        in_specs=[
            pl.BlockSpec(memory_space=pl.ANY),
            pl.BlockSpec(memory_space=pl.ANY),
            pl.BlockSpec(memory_space=pltpu.SMEM),
            pl.BlockSpec(memory_space=pltpu.SMEM),
        ],
        out_specs=[pl.BlockSpec(memory_space=pl.ANY)] * 2,
        scratch_shapes=[
            vm(NV, 40, 384), vm(NV, 40, 640),
            vm(NV, 32, 256), vm(NV, 32, 256), vm(NV, 32, 256),
            vm(NV, 32, 512), vm(NV, 32, 512),
            vm(NV, 2, 8, 256), vm(NV, 2, 16, 128),
            vm(16, 512), vm(320, 128), vm(4, 160, 128),
            vm(128, 512), vm(256, 128), vm(512, 128), vm(128, 128),
            vm(GY, 24, 128), vm(GY, 24, 128),
            vm(GY, 16, 128), vm(GY, 16, 128), vm(GY, 16, 128), vm(GY, 16, 128),
            vm(2, 16, 256), vm(2, 16, 256), vm(2, 3, 8, 128), vm(2, 3, 8, 128),
            dma((2,)), dma((2,)),
            dma((7,)), dma((8,)), dma((7,)), dma((8,)), dma((7,)), dma((8,)), dma((7,)), dma((8,)),
            dma((4,)), dma((4,)),
        ],
        compiler_params=pltpu.CompilerParams(collective_id=0, has_side_effects=True),
        name="amr_step",
    )(coarse_state, fine_state.reshape(NV, 32, 512), slot_site, box_live)
    return coarse_out, fine_out.reshape(1, NV, 32, 512)


def solution(mesh):
    return jax.shard_map(
        shards,
        mesh=mesh,
        in_specs=(
            P(None, "gx", "gy"),
            P(("gx", "gy"), None, None, None),
            P(("gx", "gy"), None),
            P(("gx", "gy")),
        ),
        out_specs=(P(None, "gx", "gy"), P(("gx", "gy"), None, None, None)),
        check_vma=False,
    )
```

profile of v0, /device:TPU:8, one launch (start us, length us, event | category | flops | bytes accessed | tf_op | source)
XLA Modules:
  0.0 40.9 jit_solution(9408525533827363212)
XLA Ops:
  1.3 37.3 %amr_step.1 = (f32[5,32,256]{2,1,0:T(8,128)}, f32[5,32,512]{2,1,0:T(8,128)}) custom-call(f32[5,32,256]{2,1,0:T(8,128)} %coarse.1, f32[5,32,512]{2,1,0:T(8,128)} %bitcast.3, s32[1,2]{1,0:T(1,128)} %site_ref.1, s32[1]{0:T(128)S(6)} %copy.8.live_ref), custom_call_target="tpu_custom_call" | custom-call | tf_op jit(solution)/shard_map/amr_step/pallas_call | solution.py:409
  38.5 0.0 copy-start
  38.6 1.6 %copy.9 = f32[5,32,256]{2,1,0:T(8,128)} copy(f32[5,32,256]{2,1,0:T(8,128)} %get-tuple-element.8) | data formatting | bytes 327680
  40.2 0.0 copy-done
  40.2 0.7 %copy.10 = f32[1,5,32,512]{3,2,1,0:T(8,128)} copy(f32[1,5,32,512]{3,2,1,0:T(8,128)S(1)} %bitcast.2) | data formatting | bytes 655360
Async XLA Ops:
  38.5 1.7 %copy-start = (f32[5,32,512]{2,1,0:T(8,128)S(1)}, f32[5,32,512]{2,1,0:T(8,128)}, u32[]{:S(2)}) copy-start(f32[5,32,512]{2,1,0:T(8,128)} %get-tuple-element.5) | copy-start | bytes 983044
where the time goes:
time: 41.1 us; the launch traced here: 40.9 us
  Pallas kernels  37.3 us (91%)
  local copies, waits for them, and re-layouts  2.37 us (6%)
  between operations  1.29 us (3%)
    pallas_call x1, Pallas kernels, shards(): pl.pallas_call(kernel, out_shape=(jax.ShapeDtypeStruct((NV, 32, 256), F32...  37.3 us
    unnamed x4, local copies, waits for them, and re-layouts  2.37 us

commit v1 on v0

--- a/solution.py
+++ b/solution.py
@@ -98,11 +98,11 @@
 
 
 def kernel(
-    coarse, fine, site_ref, live_ref, coarse_out, fine_out,
-    cq, fq, cz, cx, cn, fz, fx, cflx, cfly, xf, yf, ps,
+    coarse, fine, site_ref, live_ref, cn, fine_out,
+    cq, fq, cz, cx, fz, fx, cflx, cfly, xf, yf, ps,
     spread_x, spread_y, gather_x, gather_y, ring, mids, pieces, stage, order, arrived,
     hxs, hxr, hys, hyr,
-    in_sem, out_sem, ring_s, ring_r, mid_s, mid_r, one_s, one_r, two_s, two_r, hal_s, hal_r,
+    in_sem, ring_s, ring_r, mid_s, mid_r, one_s, one_r, two_s, two_r, hal_s, hal_r, ready,
 ):
     gx, gy = lax.axis_index("gx"), lax.axis_index("gy")
     ngx = lax.axis_size("gx")
@@ -115,8 +115,13 @@
     load_f.start()
     barrier = pltpu.get_barrier_semaphore()
     gx_lo, gx_hi = lax.rem(gx + ngx - 1, ngx), lax.rem(gx + 1, ngx)
-    for g in (gx_lo, gx_hi):
-        pl.semaphore_signal(barrier, inc=1, device_id=(g, gy), device_id_type=MESH)
+    odd = lax.rem(gx, 2)
+
+    @pl.when(odd == 0)
+    def _():
+        for g in (gx_lo, gx_hi):
+            pl.semaphore_signal(barrier, inc=1, device_id=(g, gy), device_id_type=MESH)
+
     far = (4, 3, 5, 2, 6, 1, 7)
     peers = [lax.rem(gy + k, GY) for k in far]
     for p in peers:
@@ -192,7 +197,30 @@
                 device_id=(gx, src), device_id_type=MESH,
             ).wait_recv()
 
-    pl.semaphore_wait(barrier, 9)
+    gy_lo, gy_hi = lax.rem(gy + GY - 1, GY), lax.rem(gy + 1, GY)
+    halo = [
+        pltpu.make_async_remote_copy(
+            src_ref=src, dst_ref=dst, send_sem=hal_s.at[i], recv_sem=hal_r.at[i],
+            device_id=where, device_id_type=MESH,
+        )
+        for i, (src, dst, where) in enumerate(
+            (
+                (hxs.at[0], hxr.at[0], (gx_lo, gy)),
+                (hxs.at[1], hxr.at[1], (gx_hi, gy)),
+                (hys.at[0], hyr.at[0], (gx, gy_lo)),
+                (hys.at[1], hyr.at[1], (gx, gy_hi)),
+            )
+        )
+    ]
+    pl.semaphore_wait(barrier, 7 + 2 * odd)
+
+    @pl.when(odd == 1)
+    def _():
+        for g in (gx_lo, gx_hi):
+            pl.semaphore_signal(ready, inc=1, device_id=(g, gy), device_id_type=MESH)
+        for c in halo[:2]:
+            c.start()
+
     pending = spread(ring, ring_s, ring_r)
 
     def coarse_keep_x(m, lanes, f, low):
@@ -218,22 +246,8 @@
     )
     pending += spread(mids, mid_s, mid_r)
 
-    gy_lo, gy_hi = lax.rem(gy + GY - 1, GY), lax.rem(gy + 1, GY)
-    for i, (src, dst, where) in enumerate(
-        (
-            (hxs.at[0], hxr.at[0], (gx_lo, gy)),
-            (hxs.at[1], hxr.at[1], (gx_hi, gy)),
-            (hys.at[0], hyr.at[0], (gx, gy_lo)),
-            (hys.at[1], hyr.at[1], (gx, gy_hi)),
-        )
-    ):
-        c = pltpu.make_async_remote_copy(
-            src_ref=src, dst_ref=dst, send_sem=hal_s.at[i], recv_sem=hal_r.at[i],
-            device_id=where, device_id_type=MESH,
-        )
+    for c in halo[2:]:
         c.start()
-        pending.append(c)
-    halo = pending[-4:]
 
     site_v = jnp.full((24, 128), site, jnp.int32)
     row32 = iota((32, 128), 0)
@@ -273,8 +287,10 @@
         def emit(m, r, q, div):
             rows = pl.ds(8 * r, 8)
             new = q - courant * (fx[m, rows, :] + fz[m, rows, :] + div)
-            fq[m, rows, 0:512] = new
-            if not first:
+            if first:
+                fq[m, rows, 0:512] = new
+            else:
+                fine_out[m, rows, :] = new
                 for t in range(4):
                     ps[t, 32 * m + 8 * r : 32 * m + 8 * r + 8, :] = new[:, 128 * t : 128 * t + 128]
 
@@ -290,9 +306,6 @@
     received(mids, mid_s, mid_r)
     ghosts(mids)
     fine_step(False)
-    store_f = pltpu.make_async_copy(fq.at[:, 0:32, 0:512], fine_out, out_sem.at[0])
-    store_f.start()
-
     pairs = jnp.concatenate(
         [ps[t, pl.ds(0, 80, stride=2), :] + ps[t, pl.ds(1, 80, stride=2), :] for t in range(4)], axis=1
     )
@@ -323,6 +336,26 @@
             exchange_one(i, p, gy).start()
 
     stage[gy] = pieces[gy]
+
+    @pl.when(gy != GY - 1)
+    def _():
+        for i, k in enumerate(far):
+            exchange_one(i, gy, lax.rem(gy + GY - k, GY)).wait_recv()
+        tags = [jnp.broadcast_to(ring[s, 23:24, :], (16, 128)) for s in range(GY)]
+        for d in range(GY):
+            acc = jnp.zeros((16, 128), F32)
+            for s in range(GY):
+                acc = jnp.where(tags[s] == float(d), stage[s], acc)
+            order[d] = acc
+        for i, p in enumerate(peers):
+            exchange_two(i, p, gy).start()
+        arrived[gy] = order[gy]
+
+    @pl.when(odd == 0)
+    def _():
+        pl.semaphore_wait(ready, 2)
+        for c in halo[:2]:
+            c.start()
 
     for c in halo:
         c.wait_recv()
@@ -343,20 +376,6 @@
     w8 = weight[0:8]
     present = jnp.full((16, 128), live, jnp.int32) > 0
     row8 = iota((8, 128), 0)
-
-    @pl.when(gy != GY - 1)
-    def _():
-        for i, k in enumerate(far):
-            exchange_one(i, gy, lax.rem(gy + GY - k, GY)).wait_recv()
-        tags = [jnp.broadcast_to(ring[s, 23:24, :], (16, 128)) for s in range(GY)]
-        for d in range(GY):
-            acc = jnp.zeros((16, 128), F32)
-            for s in range(GY):
-                acc = jnp.where(tags[s] == float(d), stage[s], acc)
-            order[d] = acc
-        for i, p in enumerate(peers):
-            exchange_two(i, p, gy).start()
-        arrived[gy] = order[gy]
 
     for i, k in enumerate(far):
         src = lax.rem(gy + GY - k, GY)
@@ -385,9 +404,7 @@
             cn[m, 0:8, lanes] += jnp.where(inside & (row8 == 7), w8 * (cflx[m, 0, :, lanes] - low), 0.0)
             cn[m, 24:32, lanes] += jnp.where(inside & (row8 == 0), w8 * (high - cflx[m, 1, :, lanes]), 0.0)
 
-    store_c = pltpu.make_async_copy(cn, coarse_out, out_sem.at[1])
-    store_c.start()
-    for c in pending:
+    for c in pending + halo:
         c.wait_send()
     for i, p in enumerate(peers):
         @pl.when(p != GY - 1)
@@ -398,9 +415,6 @@
     def _():
         for i, p in enumerate(peers):
             exchange_two(i, p, gy).wait_send()
-
-    store_f.wait()
-    store_c.wait()
 
 
 def shards(coarse_state, fine_state, slot_site, box_live):
@@ -409,8 +423,8 @@
     coarse_out, fine_out = pl.pallas_call(
         kernel,
         out_shape=(
-            jax.ShapeDtypeStruct((NV, 32, 256), F32),
-            jax.ShapeDtypeStruct((NV, 32, 512), F32),
+            pltpu.VMEM((NV, 32, 256), F32),
+            pltpu.VMEM((NV, 32, 512), F32),
         ),
         in_specs=[
             pl.BlockSpec(memory_space=pl.ANY),
@@ -418,10 +432,10 @@
             pl.BlockSpec(memory_space=pltpu.SMEM),
             pl.BlockSpec(memory_space=pltpu.SMEM),
         ],
-        out_specs=[pl.BlockSpec(memory_space=pl.ANY)] * 2,
+        out_specs=[pl.BlockSpec(memory_space=pltpu.VMEM)] * 2,
         scratch_shapes=[
             vm(NV, 40, 384), vm(NV, 40, 640),
-            vm(NV, 32, 256), vm(NV, 32, 256), vm(NV, 32, 256),
+            vm(NV, 32, 256), vm(NV, 32, 256),
             vm(NV, 32, 512), vm(NV, 32, 512),
             vm(NV, 2, 8, 256), vm(NV, 2, 16, 128),
             vm(16, 512), vm(320, 128), vm(4, 160, 128),
@@ -429,9 +443,9 @@
             vm(GY, 24, 128), vm(GY, 24, 128),
             vm(GY, 16, 128), vm(GY, 16, 128), vm(GY, 16, 128), vm(GY, 16, 128),
             vm(2, 16, 256), vm(2, 16, 256), vm(2, 3, 8, 128), vm(2, 3, 8, 128),
-            dma((2,)), dma((2,)),
+            dma((2,)),
             dma((7,)), dma((8,)), dma((7,)), dma((8,)), dma((7,)), dma((8,)), dma((7,)), dma((8,)),
-            dma((4,)), dma((4,)),
+            dma((4,)), dma((4,)), pltpu.SemaphoreType.REGULAR,
         ],
         compiler_params=pltpu.CompilerParams(collective_id=0, has_side_effects=True),
         name="amr_step",

time: 41.1 us -> 34.7 us (0.84)
  Pallas kernels: 37.3 us -> 31.9 us
  local copies, waits for them, and re-layouts: 2.37 us -> 1.39 us
    pallas_call x1, Pallas kernels: 37.3 us -> 31.9 us  [shards(): pl.pallas_call(kernel, out_shape=(pltpu.VMEM((NV, 32, 256), F32), pltpu.V...]
    unnamed x4 -> x2, local copies, waits for them, and re-layouts: 2.37 us -> 1.39 us
where the time goes in v1:
time: 34.7 us; the launch traced here: 34.6 us
  Pallas kernels  31.9 us (92%)
  local copies, waits for them, and re-layouts  1.39 us (4%)
  between operations  1.29 us (4%)
    pallas_call x1, Pallas kernels, shards(): pl.pallas_call(kernel, out_shape=(pltpu.VMEM((NV, 32, 256), F32), pltpu.V...  31.9 us
    unnamed x2, local copies, waits for them, and re-layouts  1.39 us

profile of v1, /device:TPU:8, one launch (start us, length us, event | category | flops | bytes accessed | tf_op | source)
XLA Modules:
  0.0 34.6 jit_solution(16531756954594603774)
XLA Ops:
  1.3 31.9 %amr_step.1 = (f32[5,32,256]{2,1,0:T(8,128)S(1)}, f32[5,32,512]{2,1,0:T(8,128)S(1)}) custom-call(f32[5,32,256]{2,1,0:T(8,128)} %coarse.1, f32[5,32,512]{2,1,0:T(8,128)} %bitcast.3, s32[1,2]{1,0:T(1,128)} %site_ref.1, s32[1]{0:T(128)S(6)} %copy.10.live_ref), custom_call_target="tpu_custom_call" | custom-call | tf_op jit(solution)/shard_map/amr_step/pallas_call | solution.py:423
  33.2 0.7 %copy.8 = f32[5,32,256]{2,1,0:T(8,128)} copy(f32[5,32,256]{2,1,0:T(8,128)S(1)} %get-tuple-element.6) | data formatting | bytes 327680
  33.9 0.7 %copy.9 = f32[1,5,32,512]{3,2,1,0:T(8,128)} copy(f32[1,5,32,512]{3,2,1,0:T(8,128)S(1)} %bitcast.2) | data formatting | bytes 655360

commit v2 on v1

--- a/solution.py
+++ b/solution.py
@@ -98,21 +98,17 @@
 
 
 def kernel(
-    coarse, fine, site_ref, live_ref, cn, fine_out,
+    coarse, fine, site_hbm, live_ref, cn, fine_out,
     cq, fq, cz, cx, fz, fx, cflx, cfly, xf, yf, ps,
     spread_x, spread_y, gather_x, gather_y, ring, mids, pieces, stage, order, arrived,
-    hxs, hxr, hys, hyr,
-    in_sem, ring_s, ring_r, mid_s, mid_r, one_s, one_r, two_s, two_r, hal_s, hal_r, ready,
+    hxs, hxr, hys, hyr, site_ref, tags,
+    in_sem, ring_s, ring_r, mid_s, mid_r, one_s, one_r, two_s, two_r, hal_s, hal_r, tag_s, tag_r, ready,
 ):
     gx, gy = lax.axis_index("gx"), lax.axis_index("gy")
     ngx = lax.axis_size("gx")
-    site = site_ref[0, 0]
-    live = live_ref[0]
-
     load_c = pltpu.make_async_copy(coarse, cq.at[:, 0:32, 0:256], in_sem.at[0])
     load_f = pltpu.make_async_copy(fine, fq.at[:, 0:32, 0:512], in_sem.at[1])
-    load_c.start()
-    load_f.start()
+    load_s = pltpu.make_async_copy(site_hbm, site_ref, in_sem.at[2])
     barrier = pltpu.get_barrier_semaphore()
     gx_lo, gx_hi = lax.rem(gx + ngx - 1, ngx), lax.rem(gx + 1, ngx)
     odd = lax.rem(gx, 2)
@@ -126,6 +122,10 @@
     peers = [lax.rem(gy + k, GY) for k in far]
     for p in peers:
         pl.semaphore_signal(barrier, inc=1, device_id=(gx, p), device_id_type=MESH)
+
+    load_c.start()
+    load_s.start()
+    load_f.start()
 
     k, o = iota((128, 512), 0), iota((128, 512), 1)
     spread_x[...] = jnp.where(k == (o // 32) * 8 + (o % 16) // 2, 1.0, 0.0)
@@ -154,16 +154,19 @@
                 both = jnp.where(
                     iota((1, 128), 1) < 64, pltpu.roll(first, 64, 1), pltpu.roll(second, 64, 1)
                 )
-                dst[gy, 5 * face + m : 5 * face + m + 1, :] = both
+                dst[gy, m, face : face + 1, :] = both
         for face, pick in ((2, pick_low), (3, pick_high)):
             cols = jnp.concatenate([get(m, 8, 24, face - 2) for m in range(NV)], axis=0)
             copies = dot(cols, pick)
             for m in range(NV):
                 part = jnp.where(own, copies[16 * m : 16 * m + 16], 0.0)
-                dst[gy, 5 * face + m : 5 * face + m + 1, :] = jnp.sum(part, axis=0, keepdims=True)
+                dst[gy, m, face : face + 1, :] = jnp.sum(part, axis=0, keepdims=True)
 
     load_c.wait()
-    ring[gy, 16:24, :] = jnp.full((8, 128), site, jnp.int32).astype(F32)
+    load_s.wait()
+    site = site_ref[0, 0]
+    live = live_ref[0]
+    tags[gy] = jnp.full((1, 128), site, jnp.int32).astype(F32)
     put_ring(ring, lambda m, a, b, t: cq[m, a:b, 128 * t : 128 * t + 128])
     for m in range(NV):
         hxs[0, 2 * m : 2 * m + 2, :] = cq[m, 0:2, 0:256]
@@ -245,25 +248,27 @@
         * (cq[m, a:b, 128 * t : 128 * t + 128] + cn[m, a:b, 128 * t : 128 * t + 128]),
     )
     pending += spread(mids, mid_s, mid_r)
+    pending += spread(tags, tag_s, tag_r)
 
     for c in halo[2:]:
         c.start()
 
-    site_v = jnp.full((24, 128), site, jnp.int32)
+    site_v = jnp.full((NV, 4, 128), site, jnp.int32)
     row32 = iota((32, 128), 0)
     mine = iota((32, 128), 1) // 8 == row32 // 2
 
     def ghosts(buf):
-        got = jnp.zeros((24, 128), F32)
+        got = jnp.zeros((NV, 4, 128), F32)
         for s in range(GY):
             got = jnp.where(site_v == s, buf[s], got)
-        wide = dot(got[0:16], spread_x[...])
-        lows = jnp.concatenate([jnp.where(mine, got[10 + m : 11 + m], 0.0) for m in range(NV)], axis=0)
-        highs = jnp.concatenate([jnp.where(mine, got[15 + m : 16 + m], 0.0) for m in range(NV)], axis=0)
+        rows = jnp.concatenate([got[m] for m in range(NV)] + [jnp.zeros((4, 128), F32)], axis=0)
+        wide = dot(rows, spread_x[...])
+        lows = jnp.concatenate([jnp.where(mine, rows[4 * m + 2 : 4 * m + 3], 0.0) for m in range(NV)], axis=0)
+        highs = jnp.concatenate([jnp.where(mine, rows[4 * m + 3 : 4 * m + 4], 0.0) for m in range(NV)], axis=0)
         side = dot(jnp.concatenate([lows, highs], axis=1), spread_y[...])
         edge = iota((8, 512), 0) < 4
         for m in range(NV):
-            fq[m, 32:40, 0:512] = jnp.where(edge, wide[5 + m : 6 + m], wide[m : m + 1])
+            fq[m, 32:40, 0:512] = jnp.where(edge, wide[4 * m + 1 : 4 * m + 2], wide[4 * m : 4 * m + 1])
             fq[m, 0:32, 512:640] = side[32 * m : 32 * m + 32]
 
     def fine_step(first):
@@ -337,15 +342,17 @@
 
     stage[gy] = pieces[gy]
 
+    received(tags, tag_s, tag_r)
+
     @pl.when(gy != GY - 1)
     def _():
         for i, k in enumerate(far):
             exchange_one(i, gy, lax.rem(gy + GY - k, GY)).wait_recv()
-        tags = [jnp.broadcast_to(ring[s, 23:24, :], (16, 128)) for s in range(GY)]
+        owner = [jnp.broadcast_to(tags[s], (16, 128)) for s in range(GY)]
         for d in range(GY):
             acc = jnp.zeros((16, 128), F32)
             for s in range(GY):
-                acc = jnp.where(tags[s] == float(d), stage[s], acc)
+                acc = jnp.where(owner[s] == float(d), stage[s], acc)
             order[d] = acc
         for i, p in enumerate(peers):
             exchange_two(i, p, gy).start()
@@ -429,7 +436,7 @@
         in_specs=[
             pl.BlockSpec(memory_space=pl.ANY),
             pl.BlockSpec(memory_space=pl.ANY),
-            pl.BlockSpec(memory_space=pltpu.SMEM),
+            pl.BlockSpec(memory_space=pl.ANY),
             pl.BlockSpec(memory_space=pltpu.SMEM),
         ],
         out_specs=[pl.BlockSpec(memory_space=pltpu.VMEM)] * 2,
@@ -440,12 +447,13 @@
             vm(NV, 2, 8, 256), vm(NV, 2, 16, 128),
             vm(16, 512), vm(320, 128), vm(4, 160, 128),
             vm(128, 512), vm(256, 128), vm(512, 128), vm(128, 128),
-            vm(GY, 24, 128), vm(GY, 24, 128),
+            vm(GY, NV, 4, 128), vm(GY, NV, 4, 128),
             vm(GY, 16, 128), vm(GY, 16, 128), vm(GY, 16, 128), vm(GY, 16, 128),
             vm(2, 16, 256), vm(2, 16, 256), vm(2, 3, 8, 128), vm(2, 3, 8, 128),
-            dma((2,)),
+            pltpu.SMEM((1, 2), jnp.int32), vm(GY, 1, 128),
+            dma((3,)),
             dma((7,)), dma((8,)), dma((7,)), dma((8,)), dma((7,)), dma((8,)), dma((7,)), dma((8,)),
-            dma((4,)), dma((4,)), pltpu.SemaphoreType.REGULAR,
+            dma((4,)), dma((4,)), dma((7,)), dma((8,)), pltpu.SemaphoreType.REGULAR,
         ],
         compiler_params=pltpu.CompilerParams(collective_id=0, has_side_effects=True),
         name="amr_step",

time: 34.7 us -> 33.6 us (0.968)
  Pallas kernels: 31.9 us -> 30.8 us
    pallas_call x1, Pallas kernels: 31.9 us -> 30.8 us  [shards(): pl.pallas_call(kernel, out_shape=(pltpu.VMEM((NV, 32, 256), F32), pltpu.V...]
where the time goes in v2:
time: 33.6 us; the launch traced here: 33.5 us
  Pallas kernels  30.8 us (92%)
  local copies, waits for them, and re-layouts  1.39 us (4%)
  between operations  1.29 us (4%)
    pallas_call x1, Pallas kernels, shards(): pl.pallas_call(kernel, out_shape=(pltpu.VMEM((NV, 32, 256), F32), pltpu.V...  30.8 us
    unnamed x2, local copies, waits for them, and re-layouts  1.39 us

profile of v2, /device:TPU:8, one launch (start us, length us, event | category | flops | bytes accessed | tf_op | source)
XLA Modules:
  0.0 33.5 jit_solution(12159561624422705080)
XLA Ops:
  1.3 30.8 %amr_step.1 = (f32[5,32,256]{2,1,0:T(8,128)S(1)}, f32[5,32,512]{2,1,0:T(8,128)S(1)}) custom-call(f32[5,32,256]{2,1,0:T(8,128)} %coarse.1, f32[5,32,512]{2,1,0:T(8,128)} %bitcast.3, s32[1,2]{1,0:T(1,128)} %site_hbm.1, s32[1]{0:T(128)S(6)} %copy.10.live_ref), custom_call_target="tpu_custom_call" | custom-call | tf_op jit(solution)/shard_map/amr_step/pallas_call | solution.py:430
  32.1 0.7 %copy.8 = f32[5,32,256]{2,1,0:T(8,128)} copy(f32[5,32,256]{2,1,0:T(8,128)S(1)} %get-tuple-element.6) | data formatting | bytes 327680
  32.7 0.7 %copy.9 = f32[1,5,32,512]{3,2,1,0:T(8,128)} copy(f32[1,5,32,512]{3,2,1,0:T(8,128)S(1)} %bitcast.2) | data formatting | bytes 655360

commit v3 on v2

--- a/solution.py
+++ b/solution.py
@@ -12,6 +12,7 @@
 signal = (1.5, 1.3, 1.2)
 MESH = pl.DeviceIdType.MESH
 F32 = jnp.float32
+BF16 = jnp.bfloat16
 
 
 def iota(shape, dim):
@@ -94,7 +95,12 @@
 
 
 def dot(a, b):
-    return jnp.dot(a, b, precision=lax.Precision.HIGHEST, preferred_element_type=F32)
+    high = a.astype(BF16)
+    rest = a - high.astype(F32)
+    middle = rest.astype(BF16)
+    low = (rest - middle.astype(F32)).astype(BF16)
+    parts = [jnp.dot(p, b, preferred_element_type=F32) for p in (high, middle, low)]
+    return parts[0] + (parts[1] + parts[2])
 
 
 def kernel(
@@ -128,16 +134,16 @@
     load_f.start()
 
     k, o = iota((128, 512), 0), iota((128, 512), 1)
-    spread_x[...] = jnp.where(k == (o // 32) * 8 + (o % 16) // 2, 1.0, 0.0)
+    spread_x[...] = jnp.where(k == (o // 32) * 8 + (o % 16) // 2, 1.0, 0.0).astype(BF16)
     k, o = iota((256, 128), 0), iota((256, 128), 1)
     hit = (k % 8 == (o % 16) // 2) & (((k < 128) & (o >= 96)) | ((k >= 128) & (o < 32)))
-    spread_y[...] = jnp.where(hit, 1.0, 0.0)
+    spread_y[...] = jnp.where(hit, 1.0, 0.0).astype(BF16)
     k, o = iota((512, 128), 0), iota((512, 128), 1)
-    gather_x[...] = jnp.where(o == (k // 32) * 8 + (k % 16) // 2, 0.125, 0.0)
+    gather_x[...] = jnp.where(o == (k // 32) * 8 + (k % 16) // 2, 0.125, 0.0).astype(BF16)
     k, o = iota((128, 128), 0), iota((128, 128), 1)
-    gather_y[...] = jnp.where((k >= 112) & ((k % 16) // 2 == o % 8), 0.125, 0.0)
-    pick_low = jnp.where(k == 56 + o % 8, 1.0, 0.0)
-    pick_high = jnp.where(k == 64 + o % 8, 1.0, 0.0)
+    gather_y[...] = jnp.where((k >= 112) & ((k % 16) // 2 == o % 8), 0.125, 0.0).astype(BF16)
+    pick_low = jnp.where(k == 56 + o % 8, 1.0, 0.0).astype(BF16)
+    pick_high = jnp.where(k == 64 + o % 8, 1.0, 0.0).astype(BF16)
 
     cq[:, 32:40, :] = jnp.zeros((NV, 8, 384), F32)
     cq[:, 0:32, 256:384] = jnp.zeros((NV, 32, 128), F32)
@@ -446,7 +452,7 @@
             vm(NV, 32, 512), vm(NV, 32, 512),
             vm(NV, 2, 8, 256), vm(NV, 2, 16, 128),
             vm(16, 512), vm(320, 128), vm(4, 160, 128),
-            vm(128, 512), vm(256, 128), vm(512, 128), vm(128, 128),
+            *[pltpu.VMEM(s, BF16) for s in ((128, 512), (256, 128), (512, 128), (128, 128))],
             vm(GY, NV, 4, 128), vm(GY, NV, 4, 128),
             vm(GY, 16, 128), vm(GY, 16, 128), vm(GY, 16, 128), vm(GY, 16, 128),
             vm(2, 16, 256), vm(2, 16, 256), vm(2, 3, 8, 128), vm(2, 3, 8, 128),

time: 33.6 us -> 33.7 us (level)
  no operation moved by 1% of the time
where the time goes in v3:
time: 33.7 us; the launch traced here: 33.5 us
  Pallas kernels  30.8 us (91%)
  local copies, waits for them, and re-layouts  1.39 us (4%)
  between operations  1.29 us (4%)
    pallas_call x1, Pallas kernels, shards(): pl.pallas_call(kernel, out_shape=(pltpu.VMEM((NV, 32, 256), F32), pltpu.V...  30.8 us
    unnamed x2, local copies, waits for them, and re-layouts  1.39 us

profile of v3, /device:TPU:8, one launch (start us, length us, event | category | flops | bytes accessed | tf_op | source)
XLA Modules:
  0.0 33.5 jit_solution(1782935782962387938)
XLA Ops:
  1.3 30.8 %amr_step.1 = (f32[5,32,256]{2,1,0:T(8,128)S(1)}, f32[5,32,512]{2,1,0:T(8,128)S(1)}) custom-call(f32[5,32,256]{2,1,0:T(8,128)} %coarse.1, f32[5,32,512]{2,1,0:T(8,128)} %bitcast.3, s32[1,2]{1,0:T(1,128)} %site_hbm.1, s32[1]{0:T(128)S(6)} %copy.10.live_ref), custom_call_target="tpu_custom_call" | custom-call | tf_op jit(solution)/shard_map/amr_step/pallas_call | solution.py:436
  32.1 0.7 %copy.8 = f32[5,32,256]{2,1,0:T(8,128)} copy(f32[5,32,256]{2,1,0:T(8,128)S(1)} %get-tuple-element.6) | data formatting | bytes 327680
  32.8 0.7 %copy.9 = f32[1,5,32,512]{3,2,1,0:T(8,128)} copy(f32[1,5,32,512]{3,2,1,0:T(8,128)S(1)} %bitcast.2) | data formatting | bytes 655360

commit v4 on v3

--- a/solution.py
+++ b/solution.py
@@ -428,6 +428,17 @@
     def _():
         for i, p in enumerate(peers):
             exchange_two(i, p, gy).wait_send()
+
+
+def write_out(coarse, fine, coarse_out, fine_out, sem):
+    copies = [
+        pltpu.make_async_copy(coarse, coarse_out, sem.at[0]),
+        pltpu.make_async_copy(fine, fine_out, sem.at[1]),
+    ]
+    for c in copies:
+        c.start()
+    for c in copies:
+        c.wait()
 
 
 def shards(coarse_state, fine_state, slot_site, box_live):
@@ -464,6 +475,17 @@
         compiler_params=pltpu.CompilerParams(collective_id=0, has_side_effects=True),
         name="amr_step",
     )(coarse_state, fine_state.reshape(NV, 32, 512), slot_site, box_live)
+    coarse_out, fine_out = pl.pallas_call(
+        write_out,
+        out_shape=(
+            jax.ShapeDtypeStruct((NV, 32, 256), F32),
+            jax.ShapeDtypeStruct((NV, 32, 512), F32),
+        ),
+        in_specs=[pl.BlockSpec(memory_space=pl.ANY)] * 2,
+        out_specs=[pl.BlockSpec(memory_space=pl.ANY)] * 2,
+        scratch_shapes=[dma((2,))],
+        name="write_out",
+    )(*[pltpu.with_memory_space_constraint(a, pltpu.VMEM) for a in (coarse_out, fine_out)])
     return coarse_out, fine_out.reshape(1, NV, 32, 512)
 
 

time: 33.7 us -> 33.1 us (0.982)
  local copies, waits for them, and re-layouts: 1.39 us -> 0 us
  Pallas kernels: 30.8 us -> 31.6 us
    unnamed x2 -> x0, local copies, waits for them, and re-layouts: 1.39 us -> none
    pallas_call x0 -> x1, Pallas kernels: none -> 0.8 us  [shards(): pl.pallas_call(write_out, out_shape=(jax.ShapeDtypeStruct((NV, 32, 256),...]
where the time goes in v4:
time: 33.1 us; the launch traced here: 32.9 us
  Pallas kernels  31.6 us (95%)
  between operations  1.28 us (4%)
    pallas_call x1, Pallas kernels, shards(): pl.pallas_call(kernel, out_shape=(pltpu.VMEM((NV, 32, 256), F32), pltpu.V...  30.8 us
    pallas_call x1, Pallas kernels, shards(): pl.pallas_call(write_out, out_shape=(jax.ShapeDtypeStruct((NV, 32, 256),...  0.8 us

profile of v4, /device:TPU:8, one launch (start us, length us, event | category | flops | bytes accessed | tf_op | source)
XLA Modules:
  0.0 32.9 jit_solution(7286379068731828308)
XLA Ops:
  1.3 30.8 %amr_step.1 = (f32[5,32,256]{2,1,0:T(8,128)S(1)}, f32[5,32,512]{2,1,0:T(8,128)S(1)}) custom-call(f32[5,32,256]{2,1,0:T(8,128)} %coarse.1, f32[5,32,512]{2,1,0:T(8,128)} %bitcast.2, s32[1,2]{1,0:T(1,128)} %site_hbm.1, s32[1]{0:T(128)S(6)} %copy.6.live_ref), custom_call_target="tpu_custom_call" | custom-call | tf_op jit(solution)/shard_map/amr_step/pallas_call | solution.py:447
  32.1 0.8 %write_out.1 = (f32[5,32,256]{2,1,0:T(8,128)}, f32[5,32,512]{2,1,0:T(8,128)}) custom-call(f32[5,32,256]{2,1,0:T(8,128)S(1)} %get-tuple-element.6.coarse, f32[5,32,512]{2,1,0:T(8,128)S(1)} %get-tuple-element.7.fine), custom_call_target="tpu_custom_call" | custom-call | tf_op jit(solution)/shard_map/write_out/pallas_call | solution.py:478
